TPU v7x, 32 devices: a whole 2x2x4 slice. The times are simulated.
32 devices in a mesh: member: 1, span: 32 (over z, y, x, core).
Axes of the slice: x: 2, y: 2, z: 4, core: 2. Of those that a mesh axis runs over, the one named last changes fastest.
Arguments:
- field: float32 [1024, 23040], P(('member', 'span')), may hold values from -60 to 60
- day_table: int32 [1024], P('member'), may hold values from 0 to 364
- band_owner: int32 [32], P('member'), may hold values from 0 to 31, as said below
- sea_mask: int32 [23040], replicated, may hold values 0 or 1
Outputs:
- coeff_out: float32 [13, 23040], P(None, ('member', 'span'))
- variance_out: float32 [23040], P(('member', 'span'))
Inputs may be any that keep to these rules, and one draw needn't show every extreme that they name: `band_owner`: a permutation of 0 to 31.
All inputs are finite; a program needn't handle non-finite values.
Results may differ from a plain program's by a relative error of at most 0.00013.
Values sent between devices are 32-bit elements; how exact they have to be, the bound alone decides.
No kernel may reach another device: no remote copies, remote signals or barrier semaphores. Data moves between devices by JAX's collectives and lax.ppermute only.
A program may use at most 64 MiB of HBM per device.

v0:
```python
import math
import jax
import jax.numpy as jnp
from jax import lax
from jax.sharding import PartitionSpec as P

HARMS = 6


def harmonic_basis(day_values):
    angles = day_values.astype(jnp.float32) * (2.0 * math.pi / 365.0)
    basis_rows = [jnp.ones_like(angles)]
    for order in range(1, HARMS + 1):
        basis_rows.append(jnp.cos(order * angles))
        basis_rows.append(jnp.sin(order * angles))
    return jnp.stack(basis_rows, 0)


def on_device(field, day_table, band_owner, sea_mask):
    groups = lax.axis_size("span")
    own_index = lax.axis_index("span")
    steps_dev, cells = field.shape
    band_cells = cells // groups
    design = harmonic_basis(day_table)
    total_steps = design.shape[1]
    gram_matrix = jnp.dot(design, design.T, precision=lax.Precision.HIGHEST)
    factor = jnp.linalg.cholesky(gram_matrix)
    slots = jnp.arange(groups, dtype=jnp.int32)
    own_band = jnp.sum(jnp.where(band_owner == own_index, slots, 0))
    source_band = jnp.sum(
        jnp.where(band_owner[None, :] == slots[:, None], slots[None, :], 0), axis=1
    )
    blocks = field.reshape(steps_dev, groups, band_cells)
    outgoing = jnp.take(blocks, source_band, axis=1).reshape(steps_dev, cells)
    weight_mask = lax.dynamic_slice_in_dim(sea_mask, own_band * band_cells, band_cells).astype(
        jnp.float32
    )
    series = lax.all_to_all(outgoing, "span", split_axis=1, concat_axis=0, tiled=True)
    projection = jnp.dot(design, series, precision=lax.Precision.HIGHEST)
    coeffs = jax.scipy.linalg.cho_solve((factor, True), projection)
    residual = series - jnp.dot(design.T, coeffs, precision=lax.Precision.HIGHEST)
    variance = jnp.sum(residual * residual, axis=0) / total_steps
    coeffs = coeffs * weight_mask[None, :]
    variance = variance * weight_mask
    return (coeffs, variance)


def solution(mesh):
    in_specs = (P(("member", "span"), None), P("member"), P("member"), P())
    out_specs = (P(None, ("member", "span")), P(("member", "span")))
    return jax.shard_map(
        on_device, mesh=mesh, in_specs=in_specs, out_specs=out_specs, check_vma=False
    )
```

profile of v0, /device:TPU:0, one launch (start us, length us, event | category | flops | bytes accessed | tf_op | source)
XLA Modules:
  0.0 103.2 jit_solution(3279304344381537644)
XLA Ops:
  0.6 0.8 select_reduce_fusion
  1.4 4.1 %reshape.51 = f32[32,32,720]{2,1,0:T(8,128)S(1)} reshape(f32[32,23040]{1,0:T(8,128)} %param.4) | data formatting | bytes 5898240 | tf_op jit(solution)/shard_map/reshape | solution.py:33
  5.6 3.5 %copy.13 = f32[32,32,720]{2,0,1:T(8,128)} copy(f32[32,32,720]{2,1,0:T(8,128)S(1)} %reshape.51) | data formatting | bytes 5898240 | tf_op jit(solution)/shard_map/reshape | solution.py:33
  9.1 2.6 %gather_fusion = f32[32,32,720]{2,1,0:T(8,128)S(1)} fusion(f32[32,32,720]{2,0,1:T(8,128)} %copy.13, s32[1024]{0:T(1024)S(1)} %pad_clamp_fusion), kind=kCustom, calls=%fused_computation | custom fusion | bytes 5898368 | tf_op jit(solution)/shard_map/jit(_take)/gather | solution.py:34
  11.7 2.0 %select_bitcast_fusion = f32[32,32,720]{2,0,1:T(8,128)} fusion(f32[32,32,720]{2,1,0:T(8,128)S(1)} %gather_fusion, pred[32]{0:T(512)(128)(4,1)S(1)} %compare_and_fusion), kind=kLoop, calls=%fused_computation.1 | loop fusion | flops 737280 | bytes 5898272 | tf_op jit(solution)/shard_map/jit(_take)/select_n | solution.py:34
  13.8 7.3 %all-to-all-start = ((f32[32,32,720]{2,0,1:T(8,128)}), f32[32,32,720]{2,0,1:T(8,128)S(1)}, u32[]{:S(2)}, u32[]{:S(2)}) async-start(f32[32,32,720]{2,0,1:T(8,128)} %select_bitcast_fusion), calls=%async_computation | async-start | bytes 6291456 | tf_op jit(solution)/shard_map/all_to_all | solution.py:38
  21.1 0.1 fusion.16
  21.2 0.1 stack.51
  21.3 0.2 fusion.20
  21.5 0.1 copy.12
  21.6 1.2 %cholesky.16 = f32[13,13]{1,0:T(8,128)S(1)} custom-call(f32[13,13]{1,0:T(8,128)S(1)} %fusion.5), custom_call_target="Cholesky" | custom-call | tf_op jit(solution)/shard_map/jit(cholesky)/cholesky | solution.py:27
  22.9 0.6 compare_reduce_fusion
  23.5 0.6 fusion
  24.2 1.0 custom-call.10
  25.2 0.0 copy-done.1
  25.2 0.6 fusion.18
  26.5 66.0 %all-to-all-done = f32[32,32,720]{2,0,1:T(8,128)S(1)} async-done(((f32[32,32,720]{2,0,1:T(8,128)}), f32[32,32,720]{2,0,1:T(8,128)S(1)}, u32[]{:S(2)}, u32[]{:S(2)}) %all-to-all-start) | async-done | bytes 2949152 | tf_op jit(solution)/shard_map/all_to_all | solution.py:38
  92.4 1.6 %fusion.21 = f32[13,720]{1,0:T(8,128)S(1)} fusion(f32[13,1024]{1,0:T(8,128)S(1)} %stack.51, f32[1024,720]{1,0:T(8,128)S(1)} %bitcast.40), kind=kOutput, calls=%fused_computation.46 | convolution fusion | flops 115015680 | bytes 3039808 | tf_op jit(solution)/shard_map/dot_general | solution.py:39
  94.0 2.3 %copy.14 = f32[1024,720]{0,1:T(8,128)} copy(f32[1024,720]{1,0:T(8,128)S(1)} %bitcast.41) | data formatting | bytes 5898240 | tf_op jit(solution)/shard_map/all_to_all | solution.py:38
  96.3 0.2 fusion.3
  96.6 0.2 fusion.1
  96.7 4.5 %multiply_reduce_fusion = f32[720]{0:T(1024)S(1)} fusion(f32[1024,720]{0,1:T(8,128)} %copy.14, f32[13,1024]{1,0:T(8,128)S(1)} %stack.51, f32[13,720]{1,0:T(8,128)S(1)} %fusion.1), kind=kOutput, calls=%fused_computation.2 | convolution fusion | flops 117226800 | bytes 3042688 | tf_op jit(solution)/shard_map/dot_general | solution.py:41
  101.2 1.4 %multiply_multiply_fusion = (f32[720]{0:T(1024)}, f32[720]{0:T(1024)S(1)}) fusion(f32[720]{0:T(1024)S(1)} %multiply_reduce_fusion, s32[23040]{0:T(1024)} %param.7, s32[]{:T(128)S(6)} %select_n.43), kind=kLoop, calls=%fused_computation.18 | loop fusion | flops 2160 | bytes 11524 | tf_op jit(solution)/shard_map/mul | solution.py:44
  102.6 0.6 broadcast_multiply_fusion
  (9 shorter events, 0.1 us)
Async XLA Ops:
  13.8 7.3 %copy-start = (s32[1024]{0:T(1024)S(1)}, s32[1024]{0:T(1024)}, u32[]{:S(2)}) copy-start(s32[1024]{0:T(1024)} %param.5) | copy-start | bytes 12292
  13.8 11.4 %copy-start.1 = (s32[32]{0:T(128)S(1)}, s32[32]{0:T(128)}, u32[]{:S(2)}) copy-start(s32[32]{0:T(128)} %param.6) | copy-start | bytes 388
  13.8 78.7 %all-to-all-start = ((f32[32,32,720]{2,0,1:T(8,128)}), f32[32,32,720]{2,0,1:T(8,128)S(1)}, u32[]{:S(2)}, u32[]{:S(2)}) async-start(f32[32,32,720]{2,0,1:T(8,128)} %select_bitcast_fusion), calls=%async_computation | async-start | bytes 6291456 | tf_op jit(solution)/shard_map/all_to_all | solution.py:38
where the time goes:
time: 104 us; the launch traced here: 103 us
  waiting for transfers between devices  66 us (63%)
  local copies, waits for them, and re-layouts  12.8 us (12%)
  other arithmetic  9.1 us (9%)
  starting transfers between devices  7.33 us (7%)
  matrix products  6.68 us (6%)
  between operations  1.39 us (1%)
    all_to_all x1, waiting for transfers between devices, on_device(): lax.all_to_all(outgoing, 'span', split_axis=1, concat_axis=0, tiled=True)  66 us
    reshape x2, local copies, waits for them, and re-layouts, on_device(): blocks = field.reshape(steps_dev, groups, band_cells)  7.63 us
    all_to_all x1, starting transfers between devices, on_device(): lax.all_to_all(outgoing, 'span', split_axis=1, concat_axis=0, tiled=True)  7.33 us
    dot_general x1, matrix products, on_device(): jnp.dot(design.T, coeffs, precision=lax.Precision.HIGHEST)  4.5 us
    gather x1, local copies, waits for them, and re-layouts, on_device(): outgoing = jnp.take(blocks, source_band, axis=1).reshape(steps_dev, cells)  2.64 us
    all_to_all x1, local copies, waits for them, and re-layouts, on_device(): lax.all_to_all(outgoing, 'span', split_axis=1, concat_axis=0, tiled=True)  2.3 us
  transfers between devices with their start and end apart: 1, of which 1 were waited for; matrix products, arithmetic and copies ran while one was open for 5% of the time, Pallas kernels for 0%

commit v1 on v0

--- a/solution.py
+++ b/solution.py
@@ -35,7 +35,10 @@
     weight_mask = lax.dynamic_slice_in_dim(sea_mask, own_band * band_cells, band_cells).astype(
         jnp.float32
     )
-    series = lax.all_to_all(outgoing, "span", split_axis=1, concat_axis=0, tiled=True)
+    series = jnp.concatenate(
+        lax.all_to_all(jnp.stack(jnp.split(outgoing, lax.axis_size("span"), axis=1)), "span", 0, 0),
+        axis=0,
+    )
     projection = jnp.dot(design, series, precision=lax.Precision.HIGHEST)
     coeffs = jax.scipy.linalg.cho_solve((factor, True), projection)
     residual = series - jnp.dot(design.T, coeffs, precision=lax.Precision.HIGHEST)

time: 104 us -> 133 us (1.28)
  local copies, waits for them, and re-layouts: 12.8 us -> 43.7 us
  matrix products: 6.68 us -> 4.95 us
    unnamed x4 -> x37, local copies, waits for them, and re-layouts: 0.01 us -> 22.2 us
    gather x1 -> x3, local copies, waits for them, and re-layouts: 2.64 us -> 9.1 us  [on_device(): outgoing = jnp.take(blocks, source_band, axis=1).reshape(steps_dev, cells)]
    all_to_all x1 -> x0, local copies, waits for them, and re-layouts: 2.3 us -> none  [on_device(): lax.all_to_all(outgoing, 'span', split_axis=1, concat_axis=0, tiled=True)]
    reshape x0 -> x1, local copies, waits for them, and re-layouts: none -> 2.29 us  [on_device(): jnp.concatenate(lax.all_to_all(jnp.stack(jnp.split(outgoing, lax.axis_siz...]
    dot_general x1, matrix products: 4.5 us -> 2.77 us  [on_device(): jnp.dot(design.T, coeffs, precision=lax.Precision.HIGHEST)]
    reshape x2, local copies, waits for them, and re-layouts: 7.63 us -> 8.99 us  [on_device(): blocks = field.reshape(steps_dev, groups, band_cells)]
  transfers between devices with their start and end apart: 1 -> 1, of which waited for: 1 -> 1; matrix products, arithmetic and copies ran while one was open for 5% -> 4% of each run, Pallas kernels for 0% -> 0%
where the time goes in v1:
time: 133 us
  waiting for transfers between devices  65.9 us (50%)
  local copies, waits for them, and re-layouts  43.7 us (33%)
  other arithmetic  9.15 us (7%)
  starting transfers between devices  7.51 us (6%)
  matrix products  4.95 us (4%)
  between operations  1.41 us (1%)
    all_to_all x1, waiting for transfers between devices, on_device(): lax.all_to_all(jnp.stack(jnp.split(outgoing, lax.axis_size('span'), axis=...  65.9 us
    unnamed x37, local copies, waits for them, and re-layouts  22.2 us
    gather x3, local copies, waits for them, and re-layouts, on_device(): outgoing = jnp.take(blocks, source_band, axis=1).reshape(steps_dev, cells)  9.1 us
    reshape x2, local copies, waits for them, and re-layouts, on_device(): blocks = field.reshape(steps_dev, groups, band_cells)  8.99 us
    all_to_all x1, starting transfers between devices, on_device(): lax.all_to_all(jnp.stack(jnp.split(outgoing, lax.axis_size('span'), axis=...  7.51 us
    dot_general x1, matrix products, on_device(): jnp.dot(design.T, coeffs, precision=lax.Precision.HIGHEST)  2.77 us
  transfers between devices with their start and end apart: 1, of which 1 were waited for; matrix products, arithmetic and copies ran while one was open for 4% of the time, Pallas kernels for 0%

profile of v1, /device:TPU:0, one launch (start us, length us, event | category | flops | bytes accessed | tf_op | source)
XLA Modules:
  0.0 132.6 jit_solution(13275468093757229753)
XLA Ops:
  0.6 0.8 select_reduce_fusion
  1.4 5.3 %reshape.46 = f32[32,32,720]{2,1,0:T(8,128)} reshape(f32[32,23040]{1,0:T(8,128)} %param.4) | data formatting | bytes 5898240 | tf_op jit(solution)/shard_map/reshape | solution.py:33
  6.7 3.7 %copy.46 = f32[32,32,720]{2,0,1:T(8,128)S(1)} copy(f32[32,32,720]{2,1,0:T(8,128)} %reshape.46) | data formatting | bytes 5898240 | tf_op jit(solution)/shard_map/reshape | solution.py:33
  10.4 2.4 %gather_fusion = f32[32,32,720]{2,1,0:T(8,128)} fusion(f32[32,32,720]{2,0,1:T(8,128)S(1)} %copy.46, s32[1024]{0:T(1024)S(1)} %pad_clamp_fusion), kind=kCustom, calls=%fused_computation | custom fusion | bytes 5898368 | tf_op jit(solution)/shard_map/jit(_take)/gather | solution.py:34
  12.8 3.7 %copy.47 = f32[32,32,720]{2,1,0:T(8,128)S(1)} copy(f32[32,32,720]{2,0,1:T(8,128)} %bitcast.167) | data formatting | bytes 5898240 | tf_op jit(solution)/shard_map/jit(_take)/gather | solution.py:34
  16.6 3.0 %gather.7 = f32[32,23040]{1,0:T(8,128)} reshape(f32[32,32,720]{2,1,0:T(8,128)S(1)} %copy.47) | data formatting | bytes 5898240 | tf_op jit(solution)/shard_map/jit(_take)/gather | solution.py:34
  19.7 2.1 %broadcast_select_fusion = f32[32,23040]{1,0:T(8,128)S(1)} fusion(f32[32,23040]{1,0:T(8,128)} %gather.7, pred[23040]{0:T(1024)(128)(4,1)S(1)} %broadcast_in_dim.37), kind=kLoop, calls=%fused_computation.2 | loop fusion | flops 737280 | bytes 5921280 | tf_op jit(solution)/shard_map/jit(_take)/select_n | solution.py:34
  23.9 0.7 fusion.28
  26.1 0.7 fusion.25
  28.9 0.7 fusion.21
  31.8 0.7 fusion.17
  32.6 0.7 fusion.16
  34.6 0.7 fusion.13
  36.1 0.7 fusion.11
  40.4 0.7 fusion.5
  41.8 0.7 fusion.3
  44.7 7.5 %all-to-all-start = ((f32[32,32,720]{2,1,0:T(8,128)}), f32[32,32,720]{2,1,0:T(8,128)S(1)}, u32[]{:S(2)}, u32[]{:S(2)}) async-start(f32[32,32,720]{2,1,0:T(8,128)} %fusion), calls=%async_computation | async-start | bytes 6291456 | tf_op jit(solution)/shard_map/all_to_all | solution.py:39
  52.8 1.2 cholesky.16
  55.3 1.0 custom-call.10
  57.6 65.9 %all-to-all-done = f32[32,32,720]{2,1,0:T(8,128)S(1)} async-done(((f32[32,32,720]{2,1,0:T(8,128)}), f32[32,32,720]{2,1,0:T(8,128)S(1)}, u32[]{:S(2)}, u32[]{:S(2)}) %all-to-all-start) | async-done | bytes 2949152 | tf_op jit(solution)/shard_map/all_to_all | solution.py:39
  123.5 2.3 %copy.48 = f32[1024,720]{0,1:T(8,128)} copy(f32[1024,720]{1,0:T(8,128)S(1)} %bitcast.165) | data formatting | bytes 5898240 | tf_op jit(solution)/shard_map/reshape | solution.py:38
  125.8 1.6 %fusion.53 = f32[13,720]{1,0:T(8,128)S(1)} fusion(f32[13,1024]{1,0:T(8,128)S(1)} %stack.150, f32[1024,720]{1,0:T(8,128)S(1)} %bitcast.166), kind=kOutput, calls=%fused_computation.110 | convolution fusion | flops 115015680 | bytes 3039808 | tf_op jit(solution)/shard_map/dot_general | solution.py:42
  127.8 2.8 %multiply_reduce_fusion = f32[720]{0:T(1024)S(1)} fusion(f32[1024,720]{0,1:T(8,128)S(1)} %copy-done, f32[13,1024]{1,0:T(8,128)S(1)} %stack.150, f32[13,720]{1,0:T(8,128)S(1)} %fusion.33), kind=kOutput, calls=%fused_computation.1 | convolution fusion | flops 117226800 | bytes 3042688 | tf_op jit(solution)/shard_map/dot_general | solution.py:44
  130.6 1.4 %multiply_multiply_fusion = (f32[720]{0:T(1024)}, f32[720]{0:T(1024)S(1)}) fusion(f32[720]{0:T(1024)S(1)} %multiply_reduce_fusion, s32[23040]{0:T(1024)} %param.7, s32[]{:T(128)S(6)} %select_n.42), kind=kLoop, calls=%fused_computation.82 | loop fusion | flops 2160 | bytes 11524 | tf_op jit(solution)/shard_map/mul | solution.py:47
  (47 shorter events, 20.1 us)
Async XLA Ops:
  44.7 7.5 %copy-start.1 = (s32[1024]{0:T(1024)S(1)}, s32[1024]{0:T(1024)}, u32[]{:S(2)}) copy-start(s32[1024]{0:T(1024)} %param.5) | copy-start | bytes 12292
  44.7 11.6 %copy-start.2 = (s32[32]{0:T(128)S(1)}, s32[32]{0:T(128)}, u32[]{:S(2)}) copy-start(s32[32]{0:T(128)} %param.6) | copy-start | bytes 388
  44.7 78.8 %all-to-all-start = ((f32[32,32,720]{2,1,0:T(8,128)}), f32[32,32,720]{2,1,0:T(8,128)S(1)}, u32[]{:S(2)}, u32[]{:S(2)}) async-start(f32[32,32,720]{2,1,0:T(8,128)} %fusion), calls=%async_computation | async-start | bytes 6291456 | tf_op jit(solution)/shard_map/all_to_all | solution.py:39
  125.8 2.0 %copy-start = (f32[1024,720]{0,1:T(8,128)S(1)}, f32[1024,720]{0,1:T(8,128)}, u32[]{:S(2)}) copy-start(f32[1024,720]{0,1:T(8,128)} %copy.48) | copy-start | bytes 8847364
